TPU v7x, 32 devices: a whole 2x2x4 slice. The times are simulated.
32 devices in a mesh: kpt: 2 (over y), ga: 16 (over z, x, core).
Axes of the slice: x: 2, y: 2, z: 4, core: 2. Of those that a mesh axis runs over, the one named last changes fastest.
Arguments:
- miller_index: int32 [3, 12288], P(None, 'ga'), may hold values from -12 to 12
- kpoint: float32 [6], P('kpt'), parts along dimension 0, may hold values from -0.5 to 0.5
- waves: bfloat16 [2, 256, 12288], P(None, 'kpt', 'ga'), parts along dimension 1, may hold values from -6 to 6
- species: int32 [16], replicated, may hold values from 0 to 3
- counts: int32 [16], replicated, may hold values from 1 to 8
- positions: int32 [3, 16], replicated, may hold values from 0 to 63
- radial_coef: float32 [4, 8, 16], replicated, may hold values from -4 to 4
- coupling: float32 [16, 8, 8], replicated, as said below
Outputs:
- applied: bfloat16 [2, 256, 12288], P(None, 'kpt', 'ga'), parts along dimension 1
- energy: float32 [256], P('kpt'), parts along dimension 0
There are 2 independent parts, one for each index of `kpt`. A program takes and returns all parts, laid end to end along the dimension named above; an argument that names none is the same for every part. Nothing has to cross between parts.
Inputs may be any that keep to these rules, and one draw needn't show every extreme that they name: `coupling`: symmetric in its last two dimensions.
All inputs are finite; a program needn't handle non-finite values.
Results may differ from a plain program's by a relative error of at most 0.0062.
Values may be sent and summed in bfloat16 or wider, within the bound.
A program may use at most 64 MiB of HBM per device.

v0:
```python
import math
import jax
import jax.numpy as jnp
from jax import lax
from jax.sharding import PartitionSpec as P

PROJ = 8
MGRID = 64
ATOM_BLOCK = 16


def prepare(miller_index, kpoint, terms):
    shifted = miller_index.astype(jnp.float32) + kpoint[:, None]
    squared = jnp.sum(shifted * shifted, axis=0)
    widths = 0.001 * 1.5 ** jnp.arange(terms).astype(jnp.float32)
    basis = jnp.exp(-widths[:, None] * squared[None, :])
    angular = jnp.concatenate(
        [jnp.ones_like(squared)[None], shifted / jnp.sqrt(squared + 1.0)[None]], 0
    )
    angular = jnp.concatenate([angular, angular], 0)
    return (basis, angular)


def projectors(
    first, miller_index, kpoint, basis, angular, species, counts, positions, radial_coef, scaling
):
    kinds = lax.dynamic_slice_in_dim(species, first, ATOM_BLOCK)
    numbers = lax.dynamic_slice_in_dim(counts, first, ATOM_BLOCK)
    places = lax.dynamic_slice_in_dim(positions, first, ATOM_BLOCK, 1)
    selector = (kinds[:, None] == jnp.arange(radial_coef.shape[0])[None, :]).astype(jnp.float32)
    chosen = jnp.einsum("as,sjr->ajr", selector, radial_coef, precision=lax.Precision.HIGHEST)
    radial = jnp.einsum("ajr,rg->ajg", chosen, basis, precision=lax.Precision.HIGHEST)
    active = (jnp.arange(PROJ)[None, :] < numbers[:, None]).astype(jnp.float32)
    amplitude = radial * angular[None] * active[:, :, None] * scaling
    winding = jnp.mod(jnp.sum(miller_index[:, None, :] * places[:, :, None], axis=0), MGRID)
    offset = jnp.sum(kpoint[:, None] * places.astype(jnp.float32), axis=0)
    phase = 2.0 * math.pi / MGRID * (winding.astype(jnp.float32) + offset[:, None])
    planes = miller_index.shape[1]
    real_part = (
        (amplitude * jnp.cos(phase)[:, None, :])
        .astype(jnp.bfloat16)
        .reshape(ATOM_BLOCK * PROJ, planes)
    )
    imag_part = (
        (-amplitude * jnp.sin(phase)[:, None, :])
        .astype(jnp.bfloat16)
        .reshape(ATOM_BLOCK * PROJ, planes)
    )
    return (real_part, imag_part)


def measure(real_part, imag_part, coeffs):
    over_re = jnp.einsum(
        "sg,bg->sb", real_part, coeffs[0], preferred_element_type=jnp.float32
    ) + jnp.einsum("sg,bg->sb", imag_part, coeffs[1], preferred_element_type=jnp.float32)
    over_im = jnp.einsum(
        "sg,bg->sb", real_part, coeffs[1], preferred_element_type=jnp.float32
    ) - jnp.einsum("sg,bg->sb", imag_part, coeffs[0], preferred_element_type=jnp.float32)
    return jnp.stack([over_re, over_im])


def spread(rows, real_part, imag_part):
    out_re = jnp.einsum(
        "sb,sg->bg", rows[0], real_part, preferred_element_type=jnp.float32
    ) - jnp.einsum("sb,sg->bg", rows[1], imag_part, preferred_element_type=jnp.float32)
    out_im = jnp.einsum(
        "sb,sg->bg", rows[1], real_part, preferred_element_type=jnp.float32
    ) + jnp.einsum("sb,sg->bg", rows[0], imag_part, preferred_element_type=jnp.float32)
    return jnp.stack([out_re, out_im])


def on_device(miller_index, kpoint, waves, species, counts, positions, radial_coef, coupling):
    planes = waves.shape[2]
    bands = waves.shape[1]
    scaling = 1.0 / math.sqrt(planes * lax.axis_size("ga"))
    atoms = coupling.shape[0]
    slots_all = atoms * PROJ
    blocks = atoms // ATOM_BLOCK
    width = ATOM_BLOCK * PROJ
    basis, angular = prepare(miller_index, kpoint, radial_coef.shape[2])

    def build(index):
        return projectors(
            index * ATOM_BLOCK,
            miller_index,
            kpoint,
            basis,
            angular,
            species,
            counts,
            positions,
            radial_coef,
            scaling,
        )

    empty = jnp.zeros((2, bands, planes), jnp.float32)

    def first_pass(index, table):
        real_part, imag_part = build(index)
        return lax.dynamic_update_slice_in_dim(
            table, measure(real_part, imag_part, waves), index * width, 1
        )

    local = lax.fori_loop(0, blocks, first_pass, jnp.zeros((2, slots_all, bands), jnp.float32))
    summed = lax.psum(local, "ga")
    shaped = summed.reshape(2, atoms, PROJ, summed.shape[2])
    weighted = jnp.einsum("aij,cajb->caib", coupling, shaped, precision=lax.Precision.HIGHEST)
    weighted = weighted.reshape(2, atoms * PROJ, summed.shape[2])
    energy = jnp.sum(summed * weighted, axis=(0, 1))
    table = weighted.astype(jnp.bfloat16)

    def second_pass(index, output):
        real_part, imag_part = build(index)
        rows = lax.dynamic_slice_in_dim(table, index * width, width, 1)
        return output + spread(rows, real_part, imag_part)

    output = lax.fori_loop(0, blocks, second_pass, empty)
    return (output.astype(jnp.bfloat16), energy / slots_all)


def solution(mesh):
    in_specs = (P(None, "ga"), P("kpt"), P(None, "kpt", "ga"), P(), P(), P(), P(), P())
    out_specs = (P(None, "kpt", "ga"), P("kpt"))
    return jax.shard_map(
        on_device, mesh=mesh, in_specs=in_specs, out_specs=out_specs, check_vma=False
    )
```

profile of v0, /device:TPU:8, one launch (start us, length us, event | category | flops | bytes accessed | tf_op | source)
XLA Modules:
  0.0 116.9 jit_solution(3049479459820801523)
XLA Ops:
  7.3 0.6 copy-done.6
  7.8 0.8 multiply_reduce_fusion.2
  8.6 0.8 multiply_reduce_fusion.1
  9.6 0.6 copy-done.8
  10.3 0.3 fusion.40
  10.6 0.4 copy-done.7
  10.9 0.2 fusion.33
  11.2 0.6 fusion.8
  11.8 0.4 copy-done.1
  12.2 0.2 fusion.9
  12.4 0.2 fusion.13
  12.6 0.2 fusion.5
  12.8 0.2 fusion.6
  13.1 0.7 pad_maximum_fusion.1
  13.8 0.7 copy-done.4
  14.6 91.3 %all-reduce.2.cloned.1.call-done = f32[2,128,128]{2,1,0:T(8,128)} async-done(((f32[2,128,128]{2,1,0:T(8,128)}), f32[2,128,128]{2,1,0:T(8,128)}) %all-reduce.2.cloned.1.call-update) | async-done | bytes 131088 | tf_op jit(solution)/shard_map/psum | solution.py:105
  105.9 1.1 convolution_bitcast_fusion
  107.1 0.2 fusion.30
  107.3 0.2 fusion.29
  107.6 0.7 copy-done.2
  108.3 0.5 broadcast_multiply_fusion
  108.8 0.2 fusion.3
  109.1 0.2 fusion.4
  109.3 0.8 pad_maximum_fusion
  (24 shorter events, 0.5 us)
Async XLA Ops:
  7.2 3.4 %copy-start = (f32[4,8,16]{2,1,0:T(8,128)S(1)}, f32[4,8,16]{2,1,0:T(8,128)}, u32[]{:S(2)}) copy-start(f32[4,8,16]{2,1,0:T(8,128)} %param.14) | copy-start | bytes 6148
  7.2 0.7 copy-start.6
  7.2 2.2 %copy-start.3 = (s32[3,768]{1,0:T(4,128)S(1)}, s32[3,768]{1,0:T(4,128)}, u32[]{:S(2)}) copy-start(s32[3,768]{1,0:T(4,128)} %param.8) | copy-start | bytes 27652
  7.2 98.7 %all-reduce.2.cloned.1.call-start = ((), (), s32[]{:S(2)}) async-start(), calls=%async_computation | async-start | bytes 262144 | tf_op jit(solution)/shard_map/psum | solution.py:105
  8.6 0.8 copy-start.5
  9.5 0.7 copy-start.8
  10.3 0.7 copy-start.7
  11.2 1.0 copy-start.1
  13.7 0.8 copy-start.4
  107.3 0.9 copy-start.2
Sparse Core Ops, SparseCore 0:
  13.9 92.0 all-reduce.1
where the time goes:
time: 117 us
  waiting for transfers between devices  91.4 us (78%)
  between operations  14.2 us (12%)
  other arithmetic  4.1 us (4%)
  matrix products  3.75 us (3%)
  local copies, waits for them, and re-layouts  3.45 us (3%)
    psum x1, waiting for transfers between devices, on_device(): summed = lax.psum(local, 'ga')  91.3 us
    unnamed x19, local copies, waits for them, and re-layouts  3.43 us
  transfers between devices with their start and end apart: 1, of which 1 were waited for; matrix products, arithmetic and copies ran while one was open for 0% of the time, Pallas kernels for 0%

commit v1 on v0

--- a/solution.py
+++ b/solution.py
@@ -7,6 +7,18 @@
 PROJ = 8
 MGRID = 64
 ATOM_BLOCK = 16
+
+
+def perform_samples_all(local_values):
+    small = local_values
+    n_peers_all = jax.lax.axis_size("ga")
+    for it in [q for q in (1, 2, 4, 8, 16) if q < n_peers_all]:
+        tray = []
+        for p in range(n_peers_all):
+            tray.append((p, p ^ it))
+        local_now = jax.lax.ppermute(small, "ga", tray)
+        small = small + local_now
+    return small
 
 
 def prepare(miller_index, kpoint, terms):
@@ -102,7 +114,7 @@
         )
 
     local = lax.fori_loop(0, blocks, first_pass, jnp.zeros((2, slots_all, bands), jnp.float32))
-    summed = lax.psum(local, "ga")
+    summed = perform_samples_all(local)
     shaped = summed.reshape(2, atoms, PROJ, summed.shape[2])
     weighted = jnp.einsum("aij,cajb->caib", coupling, shaped, precision=lax.Precision.HIGHEST)
     weighted = weighted.reshape(2, atoms * PROJ, summed.shape[2])

time: 117 us -> 30.7 us (0.26)
  the two profiles are of different devices: /device:TPU:8 before, /device:TPU:0 now
where the time goes in v1:
time: 30.7 us; the launch traced here: 30.4 us
  waiting for transfers between devices  12.9 us (42%)
  starting transfers between devices  8.24 us (27%)
  other arithmetic  3.51 us (11%)
  matrix products  2.85 us (9%)
  local copies, waits for them, and re-layouts  2.1 us (7%)
  between operations  0.86 us (3%)
    ppermute x4, waiting for transfers between devices, perform_samples_all(): local_now = jax.lax.ppermute(small, 'ga', tray)  12.9 us
    ppermute x4, starting transfers between devices, perform_samples_all(): local_now = jax.lax.ppermute(small, 'ga', tray)  8.24 us
    unnamed x17, local copies, waits for them, and re-layouts  2.09 us
    reduce_sum x1, other arithmetic, prepare(): squared = jnp.sum(shifted * shifted, axis=0)  0.8 us
    another operation x1, other arithmetic, spread(): return jnp.stack([out_re, out_im])  0.78 us
    reduce_sum x1, other arithmetic, projectors(): offset = jnp.sum(kpoint[:, None] * places.astype(jnp.float32), axis=0)  0.77 us
  transfers between devices with their start and end apart: 4, of which 4 were waited for; matrix products, arithmetic and copies ran while one was open for 0% of the time, Pallas kernels for 0%

profile of v1, /device:TPU:0, one launch (start us, length us, event | category | flops | bytes accessed | tf_op | source)
XLA Modules:
  0.0 30.4 jit_solution(6824349105550514421)
XLA Ops:
  0.7 0.6 %copy-done.5 = f32[3]{0:T(128)S(1)} copy-done((f32[3]{0:T(128)S(1)}, f32[3]{0:T(128)}, u32[]{:S(2)}) %copy-start.5) | copy-done | bytes 36
  1.3 0.8 %multiply_reduce_fusion.2 = f32[16]{0:T(128)S(1)} fusion(s32[3,16]{1,0:T(4,128)} %param.13, f32[3]{0:T(128)S(1)} %copy-done.5), kind=kLoop, calls=%fused_computation.64 | loop fusion | flops 128 | bytes 268 | tf_op jit(solution)/shard_map/while/body/eval_jaxpr/reduce_sum | solution.py:48
  2.1 0.8 %multiply_reduce_fusion.1 = f32[768]{0:T(1024)S(1)} fusion(s32[3,768]{1,0:T(4,128)} %param.8, f32[3]{0:T(128)S(1)} %copy-done.5), kind=kLoop, calls=%fused_computation.55 | loop fusion | flops 8448 | bytes 12300 | tf_op jit(solution)/shard_map/reduce_sum | solution.py:26
  3.1 0.6 %copy-done.7 = s32[16]{0:T(128)S(1)} copy-done((s32[16]{0:T(128)S(1)}, s32[16]{0:T(128)}, u32[]{:S(2)}) %copy-start.7) | copy-done | bytes 88
  3.8 0.3 fusion.40
  4.0 0.4 %copy-done.6 = s32[16]{0:T(128)S(1)} copy-done((s32[16]{0:T(128)S(1)}, s32[16]{0:T(128)}, u32[]{:S(2)}) %copy-start.6) | copy-done | bytes 88
  4.7 0.6 %fusion.8 = (bf16[128,768]{1,0:T(8,128)(2,1)S(1)}, bf16[128,768]{1,0:T(8,128)(2,1)S(1)}) fusion(f32[16,768]{1,0:T(8,128)S(1)} %get-tuple-element.52, f32[16,768]{1,0:T(8,128)S(1)} %get-tuple-element.53, f32[16,8]{1,0:T(8,128)S(1)} %fusion.38, f32[8,768]{1,0:T(8,128)S(1)} %pad_maximum_fusion.2, f32[768]{0:T(1024)S(1)} %multiply_reduce_fusion.1, ...), kind=kOutput, calls=%fused_computation.17 | convolution fusion | flops 19673088 | bytes 527936 | tf_op jit(solution)/shard_map/while/body/eval_jaxpr/ajr,rg->ajg/dot_general | solution.py:44
  5.2 0.4 %copy-done.1 = bf16[2,128,768]{2,1,0:T(8,128)(2,1)S(1)} copy-done((bf16[2,128,768]{2,1,0:T(8,128)(2,1)S(1)}, bf16[2,128,768]{2,1,0:T(8,128)(2,1)}, u32[]{:S(2)}) %copy-start.1) | copy-done | bytes 393240
  6.3 0.2 fusion.6
  6.5 0.6 %collective-permute-start = (f32[2,128,128]{2,1,0:T(8,128)S(1)}, f32[2,128,128]{2,1,0:T(8,128)S(1)}, u32[]{:S(2)}, u32[]{:S(2)}) collective-permute-start(f32[2,128,128]{2,1,0:T(8,128)S(1)} %pad_maximum_fusion.1), channel_id=1, source_target_pairs={{0,1},{1,0},{2,3},{3,2},{4,5},{5,4},{6,7},{7,6},{8,9},{9,8},{10,11... | collective-permute-start | bytes 393224 | tf_op jit(solution)/shard_map/ppermute | solution.py:19
  7.1 1.0 %collective-permute-done = f32[2,128,128]{2,1,0:T(8,128)S(1)} collective-permute-done((f32[2,128,128]{2,1,0:T(8,128)S(1)}, f32[2,128,128]{2,1,0:T(8,128)S(1)}, u32[]{:S(2)}, u32[]{:S(2)}) %collective-permute-start) | collective-permute-done | bytes 131104 | tf_op jit(solution)/shard_map/ppermute | solution.py:19
  8.1 2.9 %collective-permute-start.1 = (f32[2,128,128]{2,1,0:T(8,128)S(1)}, f32[2,128,128]{2,1,0:T(8,128)S(1)}, u32[]{:S(2)}, u32[]{:S(2)}) collective-permute-start(f32[2,128,128]{2,1,0:T(8,128)S(1)} %fusion.41), channel_id=1, source_target_pairs={{0,2},{1,3},{2,0},{3,1},{4,6},{5,7},{6,4},{7,5},{8,10},{9,11},{10,... | collective-permute-start | bytes 393224 | tf_op jit(solution)/shard_map/ppermute | solution.py:19
  11.0 3.8 %collective-permute-done.1 = f32[2,128,128]{2,1,0:T(8,128)S(1)} collective-permute-done((f32[2,128,128]{2,1,0:T(8,128)S(1)}, f32[2,128,128]{2,1,0:T(8,128)S(1)}, u32[]{:S(2)}, u32[]{:S(2)}) %collective-permute-start.1) | collective-permute-done | bytes 131104 | tf_op jit(solution)/shard_map/ppermute | solution.py:19
  14.9 1.9 %collective-permute-start.2 = (f32[2,128,128]{2,1,0:T(8,128)S(1)}, f32[2,128,128]{2,1,0:T(8,128)S(1)}, u32[]{:S(2)}, u32[]{:S(2)}) collective-permute-start(f32[2,128,128]{2,1,0:T(8,128)S(1)} %fusion.55), channel_id=1, source_target_pairs={{0,4},{1,5},{2,6},{3,7},{4,0},{5,1},{6,2},{7,3},{8,12},{9,13},{10,... | collective-permute-start | bytes 393224 | tf_op jit(solution)/shard_map/ppermute | solution.py:19
  16.8 3.2 %collective-permute-done.2 = f32[2,128,128]{2,1,0:T(8,128)S(1)} collective-permute-done((f32[2,128,128]{2,1,0:T(8,128)S(1)}, f32[2,128,128]{2,1,0:T(8,128)S(1)}, u32[]{:S(2)}, u32[]{:S(2)}) %collective-permute-start.2) | collective-permute-done | bytes 131104 | tf_op jit(solution)/shard_map/ppermute | solution.py:19
  19.9 2.9 %collective-permute-start.3 = (f32[2,128,128]{2,1,0:T(8,128)S(1)}, f32[2,128,128]{2,1,0:T(8,128)S(1)}, u32[]{:S(2)}, u32[]{:S(2)}) collective-permute-start(f32[2,128,128]{2,1,0:T(8,128)S(1)} %add.111), channel_id=1, source_target_pairs={{0,8},{1,9},{2,10},{3,11},{4,12},{5,13},{6,14},{7,15},{8,0},{9,1},... | collective-permute-start | bytes 393224 | tf_op jit(solution)/shard_map/ppermute | solution.py:19
  22.9 4.9 %collective-permute-done.3 = f32[2,128,128]{2,1,0:T(8,128)S(1)} collective-permute-done((f32[2,128,128]{2,1,0:T(8,128)S(1)}, f32[2,128,128]{2,1,0:T(8,128)S(1)}, u32[]{:S(2)}, u32[]{:S(2)}) %collective-permute-start.3) | collective-permute-done | bytes 131104 | tf_op jit(solution)/shard_map/ppermute | solution.py:19
  27.8 0.2 convolution_bitcast_fusion
  28.2 0.2 fusion.30
  28.4 0.2 fusion.29
  28.6 0.5 %broadcast_multiply_fusion = f32[128]{0:T(128)} fusion(f32[128]{0:T(128)S(1)} %fusion.19), kind=kLoop, calls=%fused_computation.66 | loop fusion | flops 128 | bytes 1024 | tf_op jit(solution)/shard_map/div | solution.py:130
  29.2 0.2 fusion.3
  29.4 0.2 fusion.4
  29.6 0.8 %pad_maximum_fusion = bf16[2,128,768]{2,1,0:T(8,128)(2,1)} fusion(bf16[1,128,768]{2,1,0:T(8,128)(2,1)S(1)} %fusion.3, bf16[1,128,768]{2,1,0:T(8,128)(2,1)S(1)} %fusion.4), kind=kLoop, calls=%fused_computation.13 | loop fusion | flops 196608 | bytes 786432 | tf_op jit(solution)/shard_map/while/body/eval_jaxpr/stack | solution.py:81
  (31 shorter events, 1.4 us)
Async XLA Ops:
  0.6 3.4 %copy-start = (f32[4,8,16]{2,1,0:T(8,128)S(1)}, f32[4,8,16]{2,1,0:T(8,128)}, u32[]{:S(2)}) copy-start(f32[4,8,16]{2,1,0:T(8,128)} %param.14) | copy-start | bytes 6148
  0.6 0.7 %copy-start.5 = (f32[3]{0:T(128)S(1)}, f32[3]{0:T(128)}, u32[]{:S(2)}) copy-start(f32[3]{0:T(128)} %param.9) | copy-start | bytes 40
  0.7 2.2 %copy-start.2 = (s32[3,768]{1,0:T(4,128)S(1)}, s32[3,768]{1,0:T(4,128)}, u32[]{:S(2)}) copy-start(s32[3,768]{1,0:T(4,128)} %param.8) | copy-start | bytes 27652
  2.1 0.8 %copy-start.4 = (s32[3,16]{1,0:T(4,128)S(1)}, s32[3,16]{1,0:T(4,128)}, u32[]{:S(2)}) copy-start(s32[3,16]{1,0:T(4,128)} %param.13) | copy-start | bytes 580
  3.0 0.7 %copy-start.7 = (s32[16]{0:T(128)S(1)}, s32[16]{0:T(128)}, u32[]{:S(2)}) copy-start(s32[16]{0:T(128)} %param.12) | copy-start | bytes 196
  3.8 0.7 %copy-start.6 = (s32[16]{0:T(128)S(1)}, s32[16]{0:T(128)}, u32[]{:S(2)}) copy-start(s32[16]{0:T(128)} %param.11) | copy-start | bytes 196
  4.6 1.0 %copy-start.1 = (bf16[2,128,768]{2,1,0:T(8,128)(2,1)S(1)}, bf16[2,128,768]{2,1,0:T(8,128)(2,1)}, u32[]{:S(2)}) copy-start(bf16[2,128,768]{2,1,0:T(8,128)(2,1)} %param.10) | copy-start | bytes 1179652
  6.5 1.5 %collective-permute-start = (f32[2,128,128]{2,1,0:T(8,128)S(1)}, f32[2,128,128]{2,1,0:T(8,128)S(1)}, u32[]{:S(2)}, u32[]{:S(2)}) collective-permute-start(f32[2,128,128]{2,1,0:T(8,128)S(1)} %pad_maximum_fusion.1), channel_id=1, source_target_pairs={{0,1},{1,0},{2,3},{3,2},{4,5},{5,4},{6,7},{7,6},{8,9},{9,8},{10,11... | collective-permute-start | bytes 393224 | tf_op jit(solution)/shard_map/ppermute | solution.py:19
  8.1 6.7 %collective-permute-start.1 = (f32[2,128,128]{2,1,0:T(8,128)S(1)}, f32[2,128,128]{2,1,0:T(8,128)S(1)}, u32[]{:S(2)}, u32[]{:S(2)}) collective-permute-start(f32[2,128,128]{2,1,0:T(8,128)S(1)} %fusion.41), channel_id=1, source_target_pairs={{0,2},{1,3},{2,0},{3,1},{4,6},{5,7},{6,4},{7,5},{8,10},{9,11},{10,... | collective-permute-start | bytes 393224 | tf_op jit(solution)/shard_map/ppermute | solution.py:19
  14.9 8.0 %copy-start.3 = (f32[16,8,8]{0,2,1:T(8,128)S(1)}, f32[16,8,8]{0,2,1:T(8,128)}, u32[]{:S(2)}) copy-start(f32[16,8,8]{0,2,1:T(8,128)} %param.15) | copy-start | bytes 12292
  14.9 5.0 %collective-permute-start.2 = (f32[2,128,128]{2,1,0:T(8,128)S(1)}, f32[2,128,128]{2,1,0:T(8,128)S(1)}, u32[]{:S(2)}, u32[]{:S(2)}) collective-permute-start(f32[2,128,128]{2,1,0:T(8,128)S(1)} %fusion.55), channel_id=1, source_target_pairs={{0,4},{1,5},{2,6},{3,7},{4,0},{5,1},{6,2},{7,3},{8,12},{9,13},{10,... | collective-permute-start | bytes 393224 | tf_op jit(solution)/shard_map/ppermute | solution.py:19
  19.9 7.9 %collective-permute-start.3 = (f32[2,128,128]{2,1,0:T(8,128)S(1)}, f32[2,128,128]{2,1,0:T(8,128)S(1)}, u32[]{:S(2)}, u32[]{:S(2)}) collective-permute-start(f32[2,128,128]{2,1,0:T(8,128)S(1)} %add.111), channel_id=1, source_target_pairs={{0,8},{1,9},{2,10},{3,11},{4,12},{5,13},{6,14},{7,15},{8,0},{9,1},... | collective-permute-start | bytes 393224 | tf_op jit(solution)/shard_map/ppermute | solution.py:19
